TPU v7x, 32 devices: a whole 2x2x4 slice. The times are simulated.
32 devices in a mesh: genes: 16 (over z, y, core), cols: 2 (over x).
Axes of the slice: x: 2, y: 2, z: 4, core: 2. Of those that a mesh axis runs over, the one named last changes fastest.
Arguments:
- expression: float32 [384, 40960], P(None, ('genes', 'cols')), may hold values from -200 to 200
- resample: int32 [384], replicated, may hold values from 0 to 383
- labels: int32 [40960, 300], P(('genes', 'cols')), may hold values from 0 to 1, as said below
- ref_kim: float32 [40960], P(('genes', 'cols')), may hold values from 0 to 1
Outputs:
- connectivity: float32 [40960, 300], P(('genes', 'cols'))
- preservation: float32 [2, 300], replicated
Inputs may be any that keep to these rules, and one draw needn't show every extreme that they name: `labels`: each row holds exactly one 1; every module has 32 or more genes.
All inputs are finite; a program needn't handle non-finite values.
Results may differ from a plain program's by a relative error of at most 0.0031.
Values may be sent and summed in bfloat16 or wider, within the bound.
A program may use at most 128 MiB of HBM per device.

v0:
```python
import math
import jax
import jax.numpy as jnp
from jax import lax
from jax.sharding import PartitionSpec as P

G = 40960


def standardize(expression, resample):
    boot = jnp.take(expression, resample, axis=0)
    centered = boot - jnp.mean(boot, axis=0, keepdims=True)
    total = jnp.sum(centered * centered, axis=0, keepdims=True)
    return (centered * lax.rsqrt(total + 1e-06)).astype(jnp.bfloat16)


def local_sums(connectivity, labels, ref_kim):
    member = labels.astype(jnp.float32)
    kim = jnp.sum(connectivity * member, axis=1)
    rowsum = jnp.sum(connectivity, axis=1)
    stacked = jnp.stack(
        [kim, kim * kim, ref_kim, ref_kim * ref_kim, kim * ref_kim, rowsum, jnp.ones_like(kim)],
        axis=1,
    )
    return jnp.dot(
        member.T, stacked, precision=lax.Precision.HIGHEST, preferred_element_type=jnp.float32
    )


def preserve(sums, total_genes):
    counts = sums[:, 6]
    mean_x = sums[:, 0] / (counts * counts)
    var_x = jnp.maximum(sums[:, 1] / (counts * counts * counts) - mean_x * mean_x, 0.0001)
    mean_y = sums[:, 2] / counts
    var_y = jnp.maximum(sums[:, 3] / counts - mean_y * mean_y, 0.01)
    cross = sums[:, 4] / (counts * counts) - mean_x * mean_y
    between = (sums[:, 5] - sums[:, 0]) / (counts * (total_genes - counts))
    density = (mean_x - between) * jnp.sqrt(counts / var_x)
    linked = cross * jnp.sqrt(counts / (var_x * var_y))
    return jnp.stack([density, linked], axis=0)


def tile_term(row_block, column_block, column_ids, module_count):
    scores = lax.dot_general(
        row_block, column_block, (((0,), (0,)), ((), ())), preferred_element_type=jnp.float32
    )
    squares = scores * scores
    adjacency = (squares * squares * squares).astype(jnp.bfloat16)
    member_block = (
        column_ids[:, None] == jnp.arange(module_count, dtype=jnp.int32)[None, :]
    ).astype(jnp.bfloat16)
    return jnp.dot(adjacency, member_block, preferred_element_type=jnp.float32)


def add_tiles(carried, row_block, piece, every_ids, shard_width, module_count):
    span_width = piece.shape[1]
    column_step = shard_width * math.gcd(span_width // shard_width, 8)
    steps_total = span_width // column_step

    def one_step(step_index, accumulated):
        columns = lax.dynamic_slice_in_dim(piece, step_index * column_step, column_step, 1)
        column_ids = lax.dynamic_slice_in_dim(every_ids, step_index * column_step, column_step, 0)
        return accumulated + tile_term(row_block, columns, column_ids, module_count)

    return lax.fori_loop(0, steps_total, one_step, carried)


def local(expression, resample, labels, ref_kim):
    scaled = standardize(expression, resample)
    module_count = labels.shape[1]
    shard_width = scaled.shape[1]
    module_ids = jnp.sum(labels * jnp.arange(module_count, dtype=jnp.int32)[None, :], axis=1)
    row_block = lax.all_gather(scaled, "cols", axis=1, tiled=True)
    panel_ids = lax.all_gather(module_ids, "genes", axis=0, tiled=True)
    initial = jnp.zeros((row_block.shape[1], module_count), jnp.float32)
    partial_value = add_tiles(
        initial,
        row_block,
        lax.all_gather(scaled, "genes", axis=1, tiled=True),
        panel_ids,
        shard_width,
        module_count,
    )
    connectivity = lax.psum_scatter(partial_value, "cols", scatter_dimension=0, tiled=True)
    sums = lax.psum(local_sums(connectivity, labels, ref_kim), ("genes", "cols"))
    return (connectivity, preserve(sums, G))


def solution(mesh):
    placed = (P(None, ("genes", "cols")), P(), P(("genes", "cols"), None), P(("genes", "cols")))
    return jax.shard_map(
        local,
        mesh=mesh,
        in_specs=placed,
        out_specs=(P(("genes", "cols"), None), P()),
        check_vma=False,
    )
```

profile of v0, /device:TPU:0, one launch (start us, length us, event | category | flops | bytes accessed | tf_op | source)
XLA Modules:
  0.0 391.7 jit_solution(1327400909456358095)
XLA Ops:
  7.2 0.0 copy-start
  7.2 0.0 all-gather.6.cloned.1.call-start
  7.2 0.8 compare_select_fusion
  8.0 0.7 compare_and_fusion
  8.7 0.0 copy-done
  8.8 2.7 gather_fusion
  11.5 0.0 copy-start.2
  11.5 1.9 select_reduce_fusion
  13.4 0.2 copy-done.2
  13.6 0.3 multiply_reduce_fusion
  14.0 0.0 copy-start.3
  14.0 1.3 multiply_convert_fusion
  15.2 0.0 all-gather.6.cloned.1.call-update
  15.3 0.0 all-gather.4.cloned.1.call-start
  15.3 0.7 all-gather.4.cloned.1.call-update
  16.0 0.0 reduce-scatter.2.cloned.1.call-start
  16.1 0.0 copy-done.3
  16.1 0.2 multiply_reduce_fusion.2
  16.3 23.3 %all-gather = s32[16,1,1280]{2,1,0:T(1,128)S(1)} all-gather(s32[1,1,1280]{2,1,0:T(1,128)S(1)} %reshape.229), channel_id=1, replica_groups=mesh['genes'=16,'cols'=2] {'genes'}, dimensions={0}, use_global_device_ids=true | all-gather | bytes 87040 | tf_op jit(solution)/shard_map/all_gather | solution.py:74
  39.6 10.2 %all-gather.6.cloned.1.call-done = bf16[384,2560]{1,0:T(8,128)(2,1)} async-done(((bf16[384,1280]{1,0:T(8,128)(2,1)}), bf16[384,2560]{1,0:T(8,128)(2,1)}) %all-gather.6.cloned.1.call-update) | async-done | bytes 1966096 | tf_op jit(solution)/shard_map/all_gather | solution.py:73
  49.8 122.7 %all-gather.4.cloned.1.call-done = bf16[384,20480]{1,0:T(8,128)(2,1)} async-done(((bf16[384,1280]{1,0:T(8,128)(2,1)}), bf16[384,20480]{1,0:T(8,128)(2,1)}) %all-gather.4.cloned.1.call-update) | async-done | bytes 15728656 | tf_op jit(solution)/shard_map/all_gather | solution.py:79
  172.5 124.2 %while.14 = (s32[]{:T(128)}, f32[2560,300]{0,1:T(8,128)}, bf16[384,20480]{1,0:T(8,128)(2,1)}, bf16[384,2560]{1,0:T(8,128)(2,1)}, s32[20480]{0:T(1024)S(1)}, /*index=5*/s32[]{:T(128)}, s32[]{:T(128)}, s32[]{:T(128)}, s32[]{:T(128)}) while((s32[]{:T(128)}, f32[2560,300]{0,1:T(8,128)}, bf16[384,20480]{1,0:T(8,128)(2,1)}, ...), condition=%wide.region_4.5_spmd.clone, body=%wide.region_3.4_spmd.clone.sunk | while | flops 35970764800 | bytes 120955040 | solution.py:65
  172.5 37.4 %fusion.clone.9 = bf16[2560,10240]{0,1:T(8,128)(2,1)} fusion(bf16[384,2560]{1,0:T(8,128)(2,1)} %get-tuple-element.184, bf16[384,20480]{1,0:T(8,128)(2,1)} %get-tuple-element.183, s32[]{:T(128)S(6)} %select_n.27), kind=kOutput, calls=%fused_computation.2.clone.clone.clone.clone.clone.2.clone.1 | convolution fusion | flops 20237516800 | bytes 62259204 | tf_op jit(solution)/shard_map/while/body/eval_jaxpr/dot_general | solution.py:44
  209.9 24.2 %fusion.47 = f32[2560,300]{0,1:T(8,128)} fusion(s32[10240]{0:T(1024)S(1)} %dynamic_slice.28, f32[2560,300]{0,1:T(8,128)} %get-tuple-element.173, pred[]{:T(512)S(6)} %compare.3, bf16[2560,10240]{0,1:T(8,128)(2,1)} %fusion.clone.9), kind=kOutput, calls=%fused_computation.7.clone.3 | convolution fusion | flops 15733248000 | bytes 58613760 | tf_op jit(solution)/shard_map/while/body/eval_jaxpr/dot_general | solution.py:52
  234.1 37.4 %fusion.clone.9 = bf16[2560,10240]{0,1:T(8,128)(2,1)} fusion(bf16[384,2560]{1,0:T(8,128)(2,1)} %get-tuple-element.184, bf16[384,20480]{1,0:T(8,128)(2,1)} %get-tuple-element.183, s32[]{:T(128)S(6)} %select_n.27), kind=kOutput, calls=%fused_computation.2.clone.clone.clone.clone.clone.2.clone.1 | convolution fusion | flops 20237516800 | bytes 62259204 | tf_op jit(solution)/shard_map/while/body/eval_jaxpr/dot_general | solution.py:44
  271.6 25.1 %fusion.47 = f32[2560,300]{0,1:T(8,128)} fusion(s32[10240]{0:T(1024)S(1)} %dynamic_slice.28, f32[2560,300]{0,1:T(8,128)} %get-tuple-element.173, pred[]{:T(512)S(6)} %compare.3, bf16[2560,10240]{0,1:T(8,128)(2,1)} %fusion.clone.9), kind=kOutput, calls=%fused_computation.7.clone.3 | convolution fusion | flops 15733248000 | bytes 58613760 | tf_op jit(solution)/shard_map/while/body/eval_jaxpr/dot_general | solution.py:52
  296.7 0.0 copy-start.5
  296.7 0.0 copy-start.4
  296.7 0.0 reduce-scatter.2.cloned.1.call-update
  296.7 0.7 copy-done.5
  297.4 0.0 copy-start.1
  297.4 40.6 %reduce-scatter.2.cloned.1.call-done = f32[1280,300]{0,1:T(8,128)} async-done(((f32[2560,300]{0,1:T(8,128)}), f32[1280,300]{0,1:T(8,128)}) %reduce-scatter.2.cloned.1.call-update) | async-done | bytes 1536016 | tf_op jit(solution)/shard_map/reduce_scatter | solution.py:84
  338.0 0.0 copy-done.4
  338.0 1.6 fusion.26
  339.7 0.6 stack.27
  340.3 0.6 stack.28
  340.9 0.6 stack_broadcast_in_dim.3
  341.5 1.4 stack.29
  342.9 2.1 fusion.12
  345.0 39.5 %psum.7 = f32[300,7]{0,1:T(8,128)S(1)} all-reduce(f32[300,7]{0,1:T(8,128)S(1)} %fusion.12), channel_id=1, replica_groups=mesh['genes'=16,'cols'=2] {'genes','cols'}, use_global_device_ids=true, to_apply=%region_8.9 | all-reduce | flops 2100 | bytes 16800 | tf_op jit(solution)/shard_map/psum | solution.py:85
  384.6 0.6 pad_maximum_fusion
  385.1 0.0 copy-done.1
  (14 shorter events, 0.1 us)
Async XLA Ops:
  7.2 1.6 copy-start
  7.2 42.6 %all-gather.6.cloned.1.call-start = ((), (), s32[]{:S(2)}) async-start(), calls=%async_computation.2 | async-start | bytes 2949120 | tf_op jit(solution)/shard_map/all_gather | solution.py:73
  11.5 2.1 copy-start.2
  14.0 2.1 copy-start.3
  15.3 157.2 %all-gather.4.cloned.1.call-start = ((), (), s32[]{:S(2)}) async-start(), calls=%async_computation.1 | async-start | bytes 16711680 | tf_op jit(solution)/shard_map/all_gather | solution.py:79
  16.0 322.0 %reduce-scatter.2.cloned.1.call-start = ((), (), s32[]{:S(2)}) async-start(), calls=%async_computation.3 | async-start | bytes 4669440 | tf_op jit(solution)/shard_map/reduce_scatter | solution.py:84
  296.7 0.7 copy-start.5
  296.7 41.4 %copy-start.4 = (s32[1280,300]{0,1:T(8,128)S(1)}, s32[1280,300]{0,1:T(8,128)}, u32[]{:S(2)}) copy-start(s32[1280,300]{0,1:T(8,128)} %param.8) | copy-start | bytes 4608004
  297.4 87.8 %copy-start.1 = (f32[384,1280]{1,0:T(8,128)S(1)}, f32[384,1280]{1,0:T(8,128)}, u32[]{:S(2)}) copy-start(f32[384,1280]{1,0:T(8,128)} %param.6) | copy-start | bytes 5898244
Sparse Core Ops, SparseCore 0:
  15.4 34.3 all-gather.5
  52.6 119.7 all-gather.3
  296.8 41.1 reduce-scatter.1
where the time goes:
time: 392 us
  waiting for transfers between devices  174 us (44%)
  matrix products  126 us (32%)
  blocking collectives  62.8 us (16%)
  between operations  13.9 us (4%)
  other arithmetic  7.47 us (2%)
  local copies, waits for them, and re-layouts  6.83 us (2%)
    all_gather x1, waiting for transfers between devices, local(): lax.all_gather(scaled, 'genes', axis=1, tiled=True)  123 us
    dot_general x2, matrix products, tile_term(): lax.dot_general(row_block, column_block, (((0,), (0,)), ((), ())), prefer...  74.9 us
    dot_general x2, matrix products, tile_term(): return jnp.dot(adjacency, member_block, preferred_element_type=jnp.float32)  49.3 us
    reduce_scatter x1, waiting for transfers between devices, local(): lax.psum_scatter(partial_value, 'cols', scatter_dimension=0, tiled=True)  40.6 us
    psum x1, blocking collectives, local(): lax.psum(local_sums(connectivity, labels, ref_kim), ('genes', 'cols'))  39.5 us
    all_gather x1, blocking collectives, local(): panel_ids = lax.all_gather(module_ids, 'genes', axis=0, tiled=True)  23.3 us
    all_gather x1, waiting for transfers between devices, local(): row_block = lax.all_gather(scaled, 'cols', axis=1, tiled=True)  10.2 us
  transfers between devices with their start and end apart: 3, of which 3 were waited for; matrix products, arithmetic and copies ran while one was open for 0% of the time, Pallas kernels for 0%

commit v1 on v0

--- a/solution.py
+++ b/solution.py
@@ -82,7 +82,7 @@
         module_count,
     )
     connectivity = lax.psum_scatter(partial_value, "cols", scatter_dimension=0, tiled=True)
-    sums = lax.psum(local_sums(connectivity, labels, ref_kim), ("genes", "cols"))
+    sums = lax.psum(lax.psum(local_sums(connectivity, labels, ref_kim), "cols"), "genes")
     return (connectivity, preserve(sums, G))
 
 

time: 392 us -> 419 us (1.069)
  blocking collectives: 62.8 us -> 89.9 us
    psum x1 -> x2, blocking collectives: 39.5 us -> 66.5 us  [the longest x1 59.6 us: local(): lax.psum(lax.psum(local_sums(connectivity, labels, ref_kim), 'cols'), 'ge...]
where the time goes in v1:
time: 419 us
  waiting for transfers between devices  174 us (42%)
  matrix products  126 us (30%)
  blocking collectives  89.9 us (21%)
  between operations  13.9 us (3%)
  other arithmetic  7.47 us (2%)
  local copies, waits for them, and re-layouts  6.83 us (2%)
    all_gather x1, waiting for transfers between devices, local(): lax.all_gather(scaled, 'genes', axis=1, tiled=True)  123 us
    dot_general x2, matrix products, tile_term(): lax.dot_general(row_block, column_block, (((0,), (0,)), ((), ())), prefer...  74.9 us
    psum x1, blocking collectives, local(): lax.psum(lax.psum(local_sums(connectivity, labels, ref_kim), 'cols'), 'ge...  59.6 us
    dot_general x2, matrix products, tile_term(): return jnp.dot(adjacency, member_block, preferred_element_type=jnp.float32)  49.3 us
    reduce_scatter x1, waiting for transfers between devices, local(): lax.psum_scatter(partial_value, 'cols', scatter_dimension=0, tiled=True)  40.7 us
    all_gather x1, blocking collectives, local(): panel_ids = lax.all_gather(module_ids, 'genes', axis=0, tiled=True)  23.3 us
    all_gather x1, waiting for transfers between devices, local(): row_block = lax.all_gather(scaled, 'cols', axis=1, tiled=True)  10.2 us
  transfers between devices with their start and end apart: 3, of which 3 were waited for; matrix products, arithmetic and copies ran while one was open for 0% of the time, Pallas kernels for 0%

profile of v1, /device:TPU:0, one launch (start us, length us, event | category | flops | bytes accessed | tf_op | source)
XLA Modules:
  0.0 418.8 jit_solution(10145371595349270236)
XLA Ops:
  7.2 0.0 copy-start
  7.2 0.0 all-gather.6.cloned.1.call-start
  7.2 0.8 compare_select_fusion
  8.0 0.7 compare_and_fusion
  8.7 0.0 copy-done
  8.8 2.7 gather_fusion
  11.5 0.0 copy-start.2
  11.5 1.9 select_reduce_fusion
  13.4 0.2 copy-done.2
  13.6 0.3 multiply_reduce_fusion
  14.0 0.0 copy-start.3
  14.0 1.3 multiply_convert_fusion
  15.2 0.0 all-gather.6.cloned.1.call-update
  15.3 0.0 all-gather.4.cloned.1.call-start
  15.3 0.7 all-gather.4.cloned.1.call-update
  16.0 0.0 reduce-scatter.2.cloned.1.call-start
  16.1 0.0 copy-done.3
  16.1 0.2 multiply_reduce_fusion.2
  16.3 23.3 %all-gather = s32[16,1,1280]{2,1,0:T(1,128)S(1)} all-gather(s32[1,1,1280]{2,1,0:T(1,128)S(1)} %reshape.229), channel_id=1, replica_groups=mesh['genes'=16,'cols'=2] {'genes'}, dimensions={0}, use_global_device_ids=true | all-gather | bytes 87040 | tf_op jit(solution)/shard_map/all_gather | solution.py:74
  39.6 10.2 %all-gather.6.cloned.1.call-done = bf16[384,2560]{1,0:T(8,128)(2,1)} async-done(((bf16[384,1280]{1,0:T(8,128)(2,1)}), bf16[384,2560]{1,0:T(8,128)(2,1)}) %all-gather.6.cloned.1.call-update) | async-done | bytes 1966096 | tf_op jit(solution)/shard_map/all_gather | solution.py:73
  49.8 122.7 %all-gather.4.cloned.1.call-done = bf16[384,20480]{1,0:T(8,128)(2,1)} async-done(((bf16[384,1280]{1,0:T(8,128)(2,1)}), bf16[384,20480]{1,0:T(8,128)(2,1)}) %all-gather.4.cloned.1.call-update) | async-done | bytes 15728656 | tf_op jit(solution)/shard_map/all_gather | solution.py:79
  172.5 124.2 %while.14 = (s32[]{:T(128)}, f32[2560,300]{0,1:T(8,128)}, bf16[384,20480]{1,0:T(8,128)(2,1)}, bf16[384,2560]{1,0:T(8,128)(2,1)}, s32[20480]{0:T(1024)S(1)}, /*index=5*/s32[]{:T(128)}, s32[]{:T(128)}, s32[]{:T(128)}, s32[]{:T(128)}) while((s32[]{:T(128)}, f32[2560,300]{0,1:T(8,128)}, bf16[384,20480]{1,0:T(8,128)(2,1)}, ...), condition=%wide.region_4.5_spmd.clone, body=%wide.region_3.4_spmd.clone.sunk | while | flops 35970764800 | bytes 120955040 | solution.py:65
  172.5 37.4 %fusion.clone.9 = bf16[2560,10240]{0,1:T(8,128)(2,1)} fusion(bf16[384,2560]{1,0:T(8,128)(2,1)} %get-tuple-element.184, bf16[384,20480]{1,0:T(8,128)(2,1)} %get-tuple-element.183, s32[]{:T(128)S(6)} %select_n.27), kind=kOutput, calls=%fused_computation.2.clone.clone.clone.clone.clone.2.clone.1 | convolution fusion | flops 20237516800 | bytes 62259204 | tf_op jit(solution)/shard_map/while/body/eval_jaxpr/dot_general | solution.py:44
  209.9 24.2 %fusion.47 = f32[2560,300]{0,1:T(8,128)} fusion(s32[10240]{0:T(1024)S(1)} %dynamic_slice.28, f32[2560,300]{0,1:T(8,128)} %get-tuple-element.173, pred[]{:T(512)S(6)} %compare.3, bf16[2560,10240]{0,1:T(8,128)(2,1)} %fusion.clone.9), kind=kOutput, calls=%fused_computation.7.clone.3 | convolution fusion | flops 15733248000 | bytes 58613760 | tf_op jit(solution)/shard_map/while/body/eval_jaxpr/dot_general | solution.py:52
  234.1 37.4 %fusion.clone.9 = bf16[2560,10240]{0,1:T(8,128)(2,1)} fusion(bf16[384,2560]{1,0:T(8,128)(2,1)} %get-tuple-element.184, bf16[384,20480]{1,0:T(8,128)(2,1)} %get-tuple-element.183, s32[]{:T(128)S(6)} %select_n.27), kind=kOutput, calls=%fused_computation.2.clone.clone.clone.clone.clone.2.clone.1 | convolution fusion | flops 20237516800 | bytes 62259204 | tf_op jit(solution)/shard_map/while/body/eval_jaxpr/dot_general | solution.py:44
  271.6 25.1 %fusion.47 = f32[2560,300]{0,1:T(8,128)} fusion(s32[10240]{0:T(1024)S(1)} %dynamic_slice.28, f32[2560,300]{0,1:T(8,128)} %get-tuple-element.173, pred[]{:T(512)S(6)} %compare.3, bf16[2560,10240]{0,1:T(8,128)(2,1)} %fusion.clone.9), kind=kOutput, calls=%fused_computation.7.clone.3 | convolution fusion | flops 15733248000 | bytes 58613760 | tf_op jit(solution)/shard_map/while/body/eval_jaxpr/dot_general | solution.py:52
  296.7 0.0 copy-start.5
  296.7 0.0 copy-start.4
  296.7 0.0 reduce-scatter.2.cloned.1.call-update
  296.7 0.7 copy-done.5
  297.4 0.0 copy-start.1
  297.4 40.7 %reduce-scatter.2.cloned.1.call-done = f32[1280,300]{0,1:T(8,128)} async-done(((f32[2560,300]{0,1:T(8,128)}), f32[1280,300]{0,1:T(8,128)}) %reduce-scatter.2.cloned.1.call-update) | async-done | bytes 1536016 | tf_op jit(solution)/shard_map/reduce_scatter | solution.py:84
  338.1 0.0 copy-done.4
  338.1 1.6 fusion.26
  339.8 0.6 stack.27
  340.4 0.6 stack.28
  340.9 0.6 stack_broadcast_in_dim.3
  341.5 1.4 stack.29
  342.9 2.1 fusion.12
  345.0 7.0 %psum.14 = f32[300,7]{0,1:T(8,128)S(1)} all-reduce(f32[300,7]{0,1:T(8,128)S(1)} %fusion.12), channel_id=1, replica_groups=mesh['genes'=16,'cols'=2] {'cols'}, use_global_device_ids=true, to_apply=%region_8.9 | all-reduce | flops 2100 | bytes 16800 | tf_op jit(solution)/shard_map/psum | solution.py:85
  352.0 59.6 %psum.15 = f32[300,7]{0,1:T(8,128)S(1)} all-reduce(f32[300,7]{0,1:T(8,128)S(1)} %psum.14), channel_id=1, replica_groups=mesh['genes'=16,'cols'=2] {'genes'}, use_global_device_ids=true, to_apply=%region_9.10 | all-reduce | flops 2100 | bytes 16800 | tf_op jit(solution)/shard_map/psum | solution.py:85
  411.6 0.6 pad_maximum_fusion
  412.2 0.0 copy-done.1
  (14 shorter events, 0.1 us)
Async XLA Ops:
  7.2 1.6 copy-start
  7.2 42.6 %all-gather.6.cloned.1.call-start = ((), (), s32[]{:S(2)}) async-start(), calls=%async_computation.2 | async-start | bytes 2949120 | tf_op jit(solution)/shard_map/all_gather | solution.py:73
  11.5 2.1 copy-start.2
  14.0 2.1 copy-start.3
  15.3 157.2 %all-gather.4.cloned.1.call-start = ((), (), s32[]{:S(2)}) async-start(), calls=%async_computation.1 | async-start | bytes 16711680 | tf_op jit(solution)/shard_map/all_gather | solution.py:79
  16.0 322.1 %reduce-scatter.2.cloned.1.call-start = ((), (), s32[]{:S(2)}) async-start(), calls=%async_computation.3 | async-start | bytes 4669440 | tf_op jit(solution)/shard_map/reduce_scatter | solution.py:84
  296.7 0.7 copy-start.5
  296.7 41.4 %copy-start.4 = (s32[1280,300]{0,1:T(8,128)S(1)}, s32[1280,300]{0,1:T(8,128)}, u32[]{:S(2)}) copy-start(s32[1280,300]{0,1:T(8,128)} %param.8) | copy-start | bytes 4608004
  297.4 114.8 %copy-start.1 = (f32[384,1280]{1,0:T(8,128)S(1)}, f32[384,1280]{1,0:T(8,128)}, u32[]{:S(2)}) copy-start(f32[384,1280]{1,0:T(8,128)} %param.6) | copy-start | bytes 5898244
Sparse Core Ops, SparseCore 0:
  15.4 34.3 all-gather.5
  52.6 119.7 all-gather.3
  296.8 41.1 reduce-scatter.1
